TPU v7x, 128 devices: a whole 4x4x4 slice. The times are simulated.
128 devices in a mesh: tok: 16 (over z_lo, y, core), blk: 8 (over x, z_hi).
Axes of the slice: x: 4, y: 4, z: 4 (z_hi: 2, z_lo: 2; z = z_hi * 2 + z_lo), core: 2. Of those that a mesh axis runs over, the one named last changes fastest.
Arguments:
- activations: bfloat16 [8192, 4096], P('tok', 'blk'), may hold values from -52 to 52, as said below
- out_grads: bfloat16 [8192, 4096], P('tok', 'blk'), may hold values from -52 to 52, as said below
Outputs:
- act_inverse: float32 [4096, 4096], P(('tok', 'blk'))
- grad_inverse: float32 [4096, 4096], P(('tok', 'blk'))
Inputs may be any that keep to these rules, and one draw needn't show every extreme that they name: `activations`: real entries. `out_grads`: real entries.
All inputs are finite; a program needn't handle non-finite values.
Results may differ from a plain program's by a relative error of at most 0.02.
Values may be sent and summed in bfloat16 or wider, within the bound.
A program may use at most 64 MiB of HBM per device.

v0:
```python
import jax
import jax.numpy as jnp
from jax import lax
from jax.sharding import PartitionSpec as P

D = 4096
damping = 0.3
epsilon = 1e-06
divisor = 2.0


def laid_out(pieces, dim):
    pieces = jnp.moveaxis(pieces, 0, dim)
    dims = pieces.shape
    return pieces.reshape(*dims[:dim], dims[dim] * dims[dim + 1], *dims[dim + 2 :])


def sent_to_all(value, axis):
    length = lax.axis_size(axis)
    return lax.all_to_all(
        jnp.broadcast_to(value[None], (length, *value.shape)), axis, 0, 0, tiled=True
    )


def gather_directly(value, axis, dim):
    return laid_out(sent_to_all(value, axis), dim)


def side_by_side(arrays, axis, dim, along):
    widths = [a.shape[along] for a in arrays]
    both = jnp.concatenate(arrays, axis=along)
    out = lax.all_gather(both, axis, axis=dim, tiled=True)
    return tuple(jnp.split(out, [sum(widths[:k]) for k in range(1, len(widths))], axis=along))


def of_everyone(value, axis):
    everything = sent_to_all(value, axis)
    return jnp.sum(everything.astype(jnp.float32), axis=0)


def column_squares(data):
    values = data.astype(jnp.float32)
    return jnp.sum(values * values, axis=0)


def newton_steps(scaled, identity):
    half = scaled.astype(jnp.bfloat16)
    row_block = gather_directly(half, "blk", 1)
    column_block = lax.all_gather(half, "tok", axis=0, tiled=True)
    square = jnp.dot(row_block, column_block, preferred_element_type=jnp.float32)
    square_block = gather_directly(square.astype(jnp.bfloat16), "blk", 1)
    cube = jnp.dot(square_block, column_block, preferred_element_type=jnp.float32)
    return 4.0 * identity - 6.0 * scaled + 4.0 * square - cube


def body(activations, out_grads):
    tok_count = lax.axis_size("tok")
    blk_count = lax.axis_size("blk")
    tok_id = lax.axis_index("tok")
    blk_id = lax.axis_index("blk")
    token_count = activations.shape[0] * tok_count
    tile_rows = D // tok_count
    tile_cols = D // blk_count
    full_acts, full_grads = side_by_side((activations, out_grads), "blk", 1, 0)
    sums_act, sums_grad = (
        of_everyone(column_squares(full_acts).astype(jnp.bfloat16), "tok").astype(jnp.float32),
        of_everyone(column_squares(full_grads).astype(jnp.bfloat16), "tok").astype(jnp.float32),
    )
    row_ids = tok_id * tile_rows + jnp.arange(tile_rows, dtype=jnp.int32)
    col_ids = blk_id * tile_cols + jnp.arange(tile_cols, dtype=jnp.int32)
    identity = (row_ids[:, None] == col_ids[None, :]).astype(jnp.float32)

    def damped_tile(full, local, sums):
        gram_tile = lax.psum_scatter(
            lax.dot_general(
                full, local, (((0,), (0,)), ((), ())), preferred_element_type=jnp.float32
            ).astype(jnp.bfloat16),
            "tok",
            scatter_dimension=0,
            tiled=True,
        ).astype(jnp.float32)
        inverse = lax.rsqrt(sums / token_count + epsilon)
        inverse_rows = lax.dynamic_slice_in_dim(inverse, tok_id * tile_rows, tile_rows)
        inverse_cols = lax.dynamic_slice_in_dim(inverse, blk_id * tile_cols, tile_cols)
        return (
            gram_tile / token_count * inverse_rows[:, None] * inverse_cols[None, :]
            + damping * identity
        )

    damped_act = damped_tile(full_acts, activations, sums_act)
    damped_grad = damped_tile(full_grads, out_grads, sums_grad)
    results = []
    for damped in (damped_act, damped_grad):
        scaled = damped / divisor
        result_tile = newton_steps(scaled, identity)
        results.append(
            lax.all_to_all(
                result_tile.astype(jnp.bfloat16), "blk", split_axis=0, concat_axis=1, tiled=True
            ).astype(result_tile.dtype)
        )
    return (results[0], results[1])


def solution(mesh):
    placed = (P("tok", "blk"), P("tok", "blk"))
    return jax.shard_map(
        body,
        mesh=mesh,
        in_specs=placed,
        out_specs=(P(("tok", "blk"), None), P(("tok", "blk"), None)),
        check_vma=False,
    )
```

profile of v0, /device:TPU:0, one launch (start us, length us, event | category | flops | bytes accessed | tf_op | source)
XLA Modules:
  0.0 490.7 jit_solution(2053735657801038295)
XLA Ops:
  7.2 0.0 all-gather.4.cloned.1.call-start
  7.2 2.3 pad_maximum_fusion
  9.5 0.0 all-gather.4.cloned.1.call-update
  9.6 0.0 reduce-scatter.5.cloned.1.call-start
  9.6 122.6 %all-gather.4.cloned.1.call-done = bf16[1024,4096]{1,0:T(8,128)(2,1)} async-done(((bf16[1024,512]{1,0:T(8,128)(2,1)}), bf16[1024,4096]{1,0:T(8,128)(2,1)}) %all-gather.4.cloned.1.call-update) | async-done | bytes 8388624 | tf_op jit(solution)/shard_map/all_gather | solution.py:32
  132.2 6.7 %convolution_convert_fusion = bf16[4096,512]{1,0:T(8,128)(2,1)} fusion(bf16[512,512]{1,0:T(8,128)(2,1)} %param.3, bf16[1024,4096]{1,0:T(8,128)(2,1)} %all-gather.4.cloned.1.call-done), kind=kOutput, calls=%fused_computation.2 | convolution fusion | flops 2149580800 | bytes 8912896 | tf_op jit(solution)/shard_map/dot_general | solution.py:75
  138.9 0.0 reduce-scatter.5.cloned.1.call-update
  138.9 0.0 reduce-scatter.3.cloned.1.call-start
  139.0 1.0 copy-done.2
  139.9 6.5 %convolution_convert_fusion.1 = bf16[4096,512]{1,0:T(8,128)(2,1)} fusion(bf16[512,512]{1,0:T(8,128)(2,1)S(1)} %copy-done.2, bf16[1024,4096]{1,0:T(8,128)(2,1)} %all-gather.4.cloned.1.call-done), kind=kOutput, calls=%fused_computation.3 | convolution fusion | flops 2149580800 | bytes 8912896 | tf_op jit(solution)/shard_map/dot_general | solution.py:75
  146.5 4.4 multiply_reduce_fusion
  150.8 0.2 broadcast_in_dim.15
  151.0 0.5 broadcast.79
  151.6 1.4 reduce.2
  153.0 0.7 reshape.70
  153.7 4.7 all-to-all-start.4
  158.4 0.2 broadcast_in_dim.12
  158.6 1.4 reduce.3
  160.0 0.7 reshape.68
  160.8 4.1 all-to-all-done.4
  164.9 3.6 all-to-all-start
  168.5 0.0 all-gather.6.cloned.1.call-start
  168.5 0.1 reshape.71
  168.6 0.2 convert_reduce_fusion
  168.8 0.1 dynamic_slice.15
  168.9 6.4 %all-to-all-done = bf16[16,2,2048]{2,1,0:T(2,128)(2,1)S(1)} async-done(((bf16[16,2,2048]{2,1,0:T(2,128)(2,1)}), bf16[16,2,2048]{2,1,0:T(2,128)(2,1)S(1)}, u32[]{:S(2)}, u32[]{:S(2)}) %all-to-all-start) | async-done | bytes 131104 | tf_op jit(solution)/shard_map/all_to_all | solution.py:20
  175.3 0.1 reshape.69
  175.4 0.2 convert_reduce_fusion.1
  175.6 0.1 dynamic_slice.13
  175.7 0.1 dynamic-slice_multiply_fusion
  175.8 0.1 dynamic-slice_multiply_fusion.1
  175.9 31.3 %reduce-scatter.5.cloned.1.call-done = bf16[256,512]{1,0:T(8,128)(2,1)} async-done(((bf16[4096,512]{1,0:T(8,128)(2,1)}), bf16[256,512]{1,0:T(8,128)(2,1)}) %reduce-scatter.5.cloned.1.call-update) | async-done | bytes 262160 | tf_op jit(solution)/shard_map/reduce_scatter | solution.py:74
  207.1 67.9 %reduce-scatter.3.cloned.1.call-done = bf16[256,512]{1,0:T(8,128)(2,1)} async-done(((bf16[4096,512]{1,0:T(8,128)(2,1)}), bf16[256,512]{1,0:T(8,128)(2,1)}) %reduce-scatter.3.cloned.1.call-update) | async-done | bytes 262160 | tf_op jit(solution)/shard_map/reduce_scatter | solution.py:74
  275.0 2.1 multiply_convert_fusion
  277.1 0.0 all-gather.8.cloned.1.call-start
  277.2 0.5 all-gather.8.cloned.1.call-update
  277.7 1.1 copy.27
  278.8 1.5 broadcast_in_dim.13
  280.3 6.7 %all-to-all-start.1 = ((bf16[8,256,512]{1,2,0:T(8,128)(2,1)}), bf16[8,256,512]{1,2,0:T(8,128)(2,1)S(1)}, u32[]{:S(2)}, u32[]{:S(2)}) async-start(bf16[8,256,512]{1,2,0:T(8,128)(2,1)} %broadcast_in_dim.13), calls=%async_computation.2 | async-start | bytes 4194304 | tf_op jit(solution)/shard_map/all_to_all | solution.py:20
  287.1 0.1 copy.31
  287.2 29.2 %all-to-all-done.1 = bf16[8,256,512]{1,2,0:T(8,128)(2,1)S(1)} async-done(((bf16[8,256,512]{1,2,0:T(8,128)(2,1)}), bf16[8,256,512]{1,2,0:T(8,128)(2,1)S(1)}, u32[]{:S(2)}, u32[]{:S(2)}) %all-to-all-start.1) | async-done | bytes 2097184 | tf_op jit(solution)/shard_map/all_to_all | solution.py:20
  316.4 1.6 broadcast_in_dim.16
  318.0 0.4 copy-done.1
  318.4 4.7 all-to-all-start.5
  323.1 28.8 %all-gather.6.cloned.1.call-done = bf16[4096,512]{1,0:T(8,128)(2,1)} async-done(((bf16[256,512]{1,0:T(8,128)(2,1)}), bf16[4096,512]{1,0:T(8,128)(2,1)}) %all-gather.6.cloned.1.call-update) | async-done | bytes 4194320 | tf_op jit(solution)/shard_map/all_gather | solution.py:49
  351.9 4.1 fusion.8
  356.0 0.1 copy.28
  356.1 1.5 broadcast_in_dim.14
  357.6 7.7 %all-to-all-start.2 = ((bf16[8,256,512]{1,2,0:T(8,128)(2,1)}), bf16[8,256,512]{1,2,0:T(8,128)(2,1)}, u32[]{:S(2)}, u32[]{:S(2)}) async-start(bf16[8,256,512]{1,2,0:T(8,128)(2,1)} %broadcast_in_dim.14), calls=%async_computation.3 | async-start | bytes 4194304 | tf_op jit(solution)/shard_map/all_to_all | solution.py:20
  365.3 49.7 %all-gather.8.cloned.1.call-done = bf16[4096,512]{1,0:T(8,128)(2,1)} async-done(((bf16[256,512]{1,0:T(8,128)(2,1)}), bf16[4096,512]{1,0:T(8,128)(2,1)}) %all-gather.8.cloned.1.call-update) | async-done | bytes 4194320 | tf_op jit(solution)/shard_map/all_gather | solution.py:49
  415.0 4.2 fusion.9
  419.3 0.1 copy.32
  419.4 1.5 broadcast_in_dim.17
  420.9 6.8 %all-to-all-start.6 = ((bf16[8,256,512]{1,2,0:T(8,128)(2,1)}), bf16[8,256,512]{1,2,0:T(8,128)(2,1)S(1)}, u32[]{:S(2)}, u32[]{:S(2)}) async-start(bf16[8,256,512]{1,2,0:T(8,128)(2,1)} %broadcast_in_dim.17), calls=%async_computation.8 | async-start | bytes 4194304 | tf_op jit(solution)/shard_map/all_to_all | solution.py:20
  427.7 4.9 %fusion.2 = bf16[256,512]{1,0:T(8,128)(2,1)} fusion(bf16[256,4096]{0,1:T(8,128)(2,1)} %bitcast.3, bf16[4096,512]{1,0:T(8,128)(2,1)} %all-gather.6.cloned.1.call-done, f32[256,512]{1,0:T(8,128)S(1)} %get-tuple-element.7, bf16[256,512]{1,0:T(8,128)(2,1)S(1)} %copy-done.4, f32[512]{0:T(512)S(1)} %dynamic_slice.13, f32[256]{0:T(256)S(1)} %dynamic-slice_multiply_fusion.1, ...), kind=kOutput, calls=%fused_computation.8 | convolution fusion | flops 1075445760 | bytes 7346176 | tf_op jit(solution)/shard_map/dot_general | solution.py:52
  432.6 26.9 %all-to-all-done.6 = bf16[8,256,512]{1,2,0:T(8,128)(2,1)S(1)} async-done(((bf16[8,256,512]{1,2,0:T(8,128)(2,1)}), bf16[8,256,512]{1,2,0:T(8,128)(2,1)S(1)}, u32[]{:S(2)}, u32[]{:S(2)}) %all-to-all-start.6) | async-done | bytes 2097184 | tf_op jit(solution)/shard_map/all_to_all | solution.py:20
  459.5 3.5 all-to-all-start.3
  463.1 4.3 fusion.3
  467.4 4.1 all-to-all-done.3
  471.5 3.4 all-to-all-start.7
  474.9 0.1 convert_bitcast_fusion.1
  475.0 0.8 copy.34
  475.8 7.5 %all-to-all-done.7 = bf16[8,32,512]{2,1,0:T(8,128)(2,1)S(1)} async-done(((bf16[8,32,512]{2,1,0:T(8,128)(2,1)}), bf16[8,32,512]{2,1,0:T(8,128)(2,1)S(1)}, u32[]{:S(2)}, u32[]{:S(2)}) %all-to-all-start.7) | async-done | bytes 262176 | tf_op jit(solution)/shard_map/all_to_all | solution.py:97
  483.3 0.8 copy.35
  (17 shorter events, 0.1 us)
Async XLA Ops:
  7.2 125.1 %all-gather.4.cloned.1.call-start = ((), (), s32[]{:S(2)}) async-start(), calls=%async_computation.10 | async-start | bytes 9437184 | tf_op jit(solution)/shard_map/all_gather | solution.py:32
  9.6 197.6 %reduce-scatter.5.cloned.1.call-start = ((), (), s32[]{:S(2)}) async-start(), calls=%async_computation.13 | async-start | bytes 4456448 | tf_op jit(solution)/shard_map/reduce_scatter | solution.py:74
  138.9 1.0 copy-start.2
  138.9 136.1 %reduce-scatter.3.cloned.1.call-start = ((), (), s32[]{:S(2)}) async-start(), calls=%async_computation.11 | async-start | bytes 4456448 | tf_op jit(solution)/shard_map/reduce_scatter | solution.py:74
  153.7 11.2 %all-to-all-start.4 = ((bf16[16,2,2048]{2,1,0:T(2,128)(2,1)}), bf16[16,2,2048]{2,1,0:T(2,128)(2,1)S(1)}, u32[]{:S(2)}, u32[]{:S(2)}) async-start(bf16[16,2,2048]{2,1,0:T(2,128)(2,1)} %reshape.70), calls=%async_computation.6 | async-start | bytes 262144 | tf_op jit(solution)/shard_map/all_to_all | solution.py:20
  164.9 10.4 %all-to-all-start = ((bf16[16,2,2048]{2,1,0:T(2,128)(2,1)}), bf16[16,2,2048]{2,1,0:T(2,128)(2,1)S(1)}, u32[]{:S(2)}, u32[]{:S(2)}) async-start(bf16[16,2,2048]{2,1,0:T(2,128)(2,1)} %reshape.68), calls=%async_computation.1 | async-start | bytes 262144 | tf_op jit(solution)/shard_map/all_to_all | solution.py:20
  168.5 183.4 %all-gather.6.cloned.1.call-start = ((), (), s32[]{:S(2)}) async-start(), calls=%async_computation.12 | async-start | bytes 4456448 | tf_op jit(solution)/shard_map/all_gather | solution.py:49
  277.1 10.0 %copy-start = (bf16[256,512]{1,0:T(8,128)(2,1)S(1)}, bf16[256,512]{1,0:T(8,128)(2,1)}, u32[]{:S(2)}) copy-start(bf16[256,512]{1,0:T(8,128)(2,1)} %get-tuple-element.4) | copy-start | bytes 786436
  277.1 137.9 %all-gather.8.cloned.1.call-start = ((), (), s32[]{:S(2)}) async-start(), calls=%async_computation.14 | async-start | bytes 4456448 | tf_op jit(solution)/shard_map/all_gather | solution.py:49
  280.3 36.1 %all-to-all-start.1 = ((bf16[8,256,512]{1,2,0:T(8,128)(2,1)}), bf16[8,256,512]{1,2,0:T(8,128)(2,1)S(1)}, u32[]{:S(2)}, u32[]{:S(2)}) async-start(bf16[8,256,512]{1,2,0:T(8,128)(2,1)} %broadcast_in_dim.13), calls=%async_computation.2 | async-start | bytes 4194304 | tf_op jit(solution)/shard_map/all_to_all | solution.py:20
  316.4 2.0 copy-start.1
  318.4 37.7 %all-to-all-start.5 = ((bf16[8,256,512]{1,2,0:T(8,128)(2,1)}), bf16[8,256,512]{1,2,0:T(8,128)(2,1)S(1)}, u32[]{:S(2)}, u32[]{:S(2)}) async-start(bf16[8,256,512]{1,2,0:T(8,128)(2,1)} %broadcast_in_dim.16), calls=%async_computation.7 | async-start | bytes 4194304 | tf_op jit(solution)/shard_map/all_to_all | solution.py:20
  357.6 61.8 %all-to-all-start.2 = ((bf16[8,256,512]{1,2,0:T(8,128)(2,1)}), bf16[8,256,512]{1,2,0:T(8,128)(2,1)}, u32[]{:S(2)}, u32[]{:S(2)}) async-start(bf16[8,256,512]{1,2,0:T(8,128)(2,1)} %broadcast_in_dim.14), calls=%async_computation.3 | async-start | bytes 4194304 | tf_op jit(solution)/shard_map/all_to_all | solution.py:20
  419.2 8.5 %copy-start.4 = (bf16[256,512]{1,0:T(8,128)(2,1)S(1)}, bf16[256,512]{1,0:T(8,128)(2,1)}, u32[]{:S(2)}) copy-start(bf16[256,512]{1,0:T(8,128)(2,1)} %reduce-scatter.3.cloned.1.call-done) | copy-start | bytes 786436
  420.9 38.6 %all-to-all-start.6 = ((bf16[8,256,512]{1,2,0:T(8,128)(2,1)}), bf16[8,256,512]{1,2,0:T(8,128)(2,1)S(1)}, u32[]{:S(2)}, u32[]{:S(2)}) async-start(bf16[8,256,512]{1,2,0:T(8,128)(2,1)} %broadcast_in_dim.17), calls=%async_computation.8 | async-start | bytes 4194304 | tf_op jit(solution)/shard_map/all_to_all | solution.py:20
  427.7 35.3 %copy-start.3 = (bf16[256,512]{1,0:T(8,128)(2,1)S(1)}, bf16[256,512]{1,0:T(8,128)(2,1)}, u32[]{:S(2)}) copy-start(bf16[256,512]{1,0:T(8,128)(2,1)} %reduce-scatter.5.cloned.1.call-done) | copy-start | bytes 786436
  459.5 12.0 %all-to-all-start.3 = ((bf16[8,32,512]{2,1,0:T(8,128)(2,1)}), bf16[8,32,512]{2,1,0:T(8,128)(2,1)S(1)}, u32[]{:S(2)}, u32[]{:S(2)}) async-start(bf16[8,32,512]{2,1,0:T(8,128)(2,1)} %bitcast.4), calls=%async_computation.4 | async-start | bytes 524288 | tf_op jit(solution)/shard_map/all_to_all | solution.py:97
  471.5 11.8 %all-to-all-start.7 = ((bf16[8,32,512]{2,1,0:T(8,128)(2,1)}), bf16[8,32,512]{2,1,0:T(8,128)(2,1)S(1)}, u32[]{:S(2)}, u32[]{:S(2)}) async-start(bf16[8,32,512]{2,1,0:T(8,128)(2,1)} %bitcast.10), calls=%async_computation.9 | async-start | bytes 524288 | tf_op jit(solution)/shard_map/all_to_all | solution.py:97
Sparse Core Ops, SparseCore 0:
  10.2 122.0 all-gather.3
  139.1 68.0 reduce-scatter.4
  209.5 65.4 reduce-scatter.2
  277.3 74.5 all-gather.5
  354.0 60.9 all-gather.7
where the time goes:
time: 492 us; the launch traced here: 491 us
  waiting for transfers between devices  379 us (77%)
  starting transfers between devices  41.3 us (8%)
  matrix products  30.8 us (6%)
  between operations  14 us (3%)
  local copies, waits for them, and re-layouts  13.4 us (3%)
  other arithmetic  12.2 us (2%)
    all_gather x1, waiting for transfers between devices, side_by_side(): out = lax.all_gather(both, axis, axis=dim, tiled=True)  123 us
    reduce_scatter x2, waiting for transfers between devices, damped_tile(): lax.psum_scatter(lax.dot_general(full, local, (((0,), (0,)), ((), ())), p...  99.2 us
    all_gather x2, waiting for transfers between devices, newton_steps(): column_block = lax.all_gather(half, 'tok', axis=0, tiled=True)  78.5 us
    all_to_all x6, waiting for transfers between devices, sent_to_all(): lax.all_to_all(jnp.broadcast_to(value[None], (length, *value.shape)), axi...  66.5 us
    all_to_all x6, starting transfers between devices, sent_to_all(): lax.all_to_all(jnp.broadcast_to(value[None], (length, *value.shape)), axi...  34.2 us
    dot_general x2, matrix products, damped_tile(): lax.dot_general(full, local, (((0,), (0,)), ((), ())), preferred_element_...  13.2 us
    all_to_all x2, waiting for transfers between devices, body(): lax.all_to_all(result_tile.astype(jnp.bfloat16), 'blk', split_axis=0, con...  11.6 us
  transfers between devices with their start and end apart: 13, of which 11 were waited for; matrix products, arithmetic and copies ran while one was open for 8% of the time, Pallas kernels for 0%

commit v1 on v0

--- a/solution.py
+++ b/solution.py
@@ -46,7 +46,9 @@
 def newton_steps(scaled, identity):
     half = scaled.astype(jnp.bfloat16)
     row_block = gather_directly(half, "blk", 1)
-    column_block = lax.all_gather(half, "tok", axis=0, tiled=True)
+    column_block = jnp.concatenate(
+        lax.all_to_all(jnp.stack([half] * lax.axis_size("tok")), "tok", 0, 0), axis=0
+    )
     square = jnp.dot(row_block, column_block, preferred_element_type=jnp.float32)
     square_block = gather_directly(square.astype(jnp.bfloat16), "blk", 1)
     cube = jnp.dot(square_block, column_block, preferred_element_type=jnp.float32)

time: 492 us -> 570 us (1.16)
  blocking collectives: 0 us -> 89.7 us
  starting transfers between devices: 41.3 us -> 34.8 us
  waiting for transfers between devices: 379 us -> 373 us
    all_to_all x0 -> x2, blocking collectives: none -> 89.7 us  [the longest x1 60.2 us: newton_steps(): lax.all_to_all(jnp.stack([half] * lax.axis_size('tok')), 'tok', 0, 0)]
    all_gather x2 -> x0, waiting for transfers between devices: 78.5 us -> none  [newton_steps(): column_block = lax.all_gather(half, 'tok', axis=0, tiled=True)]
    all_to_all x0 -> x1, waiting for transfers between devices: none -> 50.8 us  [newton_steps(): lax.all_to_all(jnp.stack([half] * lax.axis_size('tok')), 'tok', 0, 0)]
    all_to_all x6 -> x5, waiting for transfers between devices: 66.5 us -> 89 us  [sent_to_all(): lax.all_to_all(jnp.broadcast_to(value[None], (length, *value.shape)), axi...]
    all_to_all x6 -> x5, starting transfers between devices: 34.2 us -> 23.1 us  [sent_to_all(): lax.all_to_all(jnp.broadcast_to(value[None], (length, *value.shape)), axi...]
  transfers between devices with their start and end apart: 13 -> 11, of which waited for: 11 -> 11; matrix products, arithmetic and copies ran while one was open for 8% -> 6% of each run, Pallas kernels for 0% -> 0%
where the time goes in v1:
time: 570 us; the launch traced here: 568 us
  waiting for transfers between devices  373 us (65%)
  blocking collectives  89.7 us (16%)
  starting transfers between devices  34.8 us (6%)
  matrix products  30.7 us (5%)
  local copies, waits for them, and re-layouts  14.6 us (3%)
  between operations  14 us (2%)
  other arithmetic  11.3 us (2%)
    all_gather x1, waiting for transfers between devices, side_by_side(): out = lax.all_gather(both, axis, axis=dim, tiled=True)  123 us
    reduce_scatter x2, waiting for transfers between devices, damped_tile(): lax.psum_scatter(lax.dot_general(full, local, (((0,), (0,)), ((), ())), p...  99.2 us
    all_to_all x5, waiting for transfers between devices, sent_to_all(): lax.all_to_all(jnp.broadcast_to(value[None], (length, *value.shape)), axi...  89 us
    all_to_all x1, blocking collectives, newton_steps(): lax.all_to_all(jnp.stack([half] * lax.axis_size('tok')), 'tok', 0, 0)  60.2 us
    all_to_all x1, waiting for transfers between devices, newton_steps(): lax.all_to_all(jnp.stack([half] * lax.axis_size('tok')), 'tok', 0, 0)  50.8 us
    all_to_all x1, blocking collectives, sent_to_all(): lax.all_to_all(jnp.broadcast_to(value[None], (length, *value.shape)), axi...  29.5 us
    all_to_all x5, starting transfers between devices, sent_to_all(): lax.all_to_all(jnp.broadcast_to(value[None], (length, *value.shape)), axi...  23.1 us
    dot_general x2, matrix products, damped_tile(): lax.dot_general(full, local, (((0,), (0,)), ((), ())), preferred_element_...  13.2 us
  transfers between devices with their start and end apart: 11, of which 11 were waited for; matrix products, arithmetic and copies ran while one was open for 6% of the time, Pallas kernels for 0%

profile of v1, /device:TPU:0, one launch (start us, length us, event | category | flops | bytes accessed | tf_op | source)
XLA Modules:
  0.0 568.3 jit_solution(3822521726182024350)
XLA Ops:
  7.2 0.0 all-gather.2.cloned.1.call-start
  7.2 2.3 pad_maximum_fusion
  9.5 0.0 all-gather.2.cloned.1.call-update
  9.6 0.0 reduce-scatter.5.cloned.1.call-start
  9.6 122.6 %all-gather.2.cloned.1.call-done = bf16[1024,4096]{1,0:T(8,128)(2,1)} async-done(((bf16[1024,512]{1,0:T(8,128)(2,1)}), bf16[1024,4096]{1,0:T(8,128)(2,1)}) %all-gather.2.cloned.1.call-update) | async-done | bytes 8388624 | tf_op jit(solution)/shard_map/all_gather | solution.py:32
  132.2 6.7 %convolution_convert_fusion = bf16[4096,512]{1,0:T(8,128)(2,1)} fusion(bf16[512,512]{1,0:T(8,128)(2,1)} %param.3, bf16[1024,4096]{1,0:T(8,128)(2,1)} %all-gather.2.cloned.1.call-done), kind=kOutput, calls=%fused_computation.2 | convolution fusion | flops 2149580800 | bytes 8912896 | tf_op jit(solution)/shard_map/dot_general | solution.py:77
  138.9 0.0 reduce-scatter.5.cloned.1.call-update
  138.9 0.0 reduce-scatter.3.cloned.1.call-start
  139.0 1.0 copy-done.1
  139.9 6.5 %convolution_convert_fusion.1 = bf16[4096,512]{1,0:T(8,128)(2,1)} fusion(bf16[512,512]{1,0:T(8,128)(2,1)S(1)} %copy-done.1, bf16[1024,4096]{1,0:T(8,128)(2,1)} %all-gather.2.cloned.1.call-done), kind=kOutput, calls=%fused_computation.3 | convolution fusion | flops 2149580800 | bytes 8912896 | tf_op jit(solution)/shard_map/dot_general | solution.py:77
  146.5 4.4 multiply_reduce_fusion
  150.8 0.2 broadcast_in_dim.15
  151.0 0.5 broadcast.83
  151.5 1.4 reduce.2
  152.9 0.7 reshape.82
  153.7 4.7 all-to-all-start.5
  158.4 0.2 broadcast_in_dim.12
  158.6 1.4 reduce.3
  160.0 0.7 reshape.80
  160.7 4.1 all-to-all-done.5
  164.8 3.7 all-to-all-start
  168.5 0.1 reshape.83
  168.6 0.2 convert_reduce_fusion
  168.8 0.1 dynamic_slice.15
  168.9 6.5 %all-to-all-done = bf16[16,2,2048]{2,1,0:T(2,128)(2,1)S(1)} async-done(((bf16[16,2,2048]{2,1,0:T(2,128)(2,1)}), bf16[16,2,2048]{2,1,0:T(2,128)(2,1)S(1)}, u32[]{:S(2)}, u32[]{:S(2)}) %all-to-all-start) | async-done | bytes 131104 | tf_op jit(solution)/shard_map/all_to_all | solution.py:20
  175.4 0.1 reshape.81
  175.5 0.2 convert_reduce_fusion.1
  175.7 0.1 dynamic_slice.13
  175.8 0.1 dynamic-slice_multiply_fusion
  175.8 31.3 %reduce-scatter.5.cloned.1.call-done = bf16[256,512]{1,0:T(8,128)(2,1)} async-done(((bf16[4096,512]{1,0:T(8,128)(2,1)}), bf16[256,512]{1,0:T(8,128)(2,1)}) %reduce-scatter.5.cloned.1.call-update) | async-done | bytes 262160 | tf_op jit(solution)/shard_map/reduce_scatter | solution.py:76
  207.1 67.9 %reduce-scatter.3.cloned.1.call-done = bf16[256,512]{1,0:T(8,128)(2,1)} async-done(((bf16[4096,512]{1,0:T(8,128)(2,1)}), bf16[256,512]{1,0:T(8,128)(2,1)}) %reduce-scatter.3.cloned.1.call-update) | async-done | bytes 262160 | tf_op jit(solution)/shard_map/reduce_scatter | solution.py:76
  275.0 1.3 multiply_convert_fusion
  276.3 0.1 copy.27
  276.5 1.5 broadcast_in_dim.13
  277.9 6.7 %all-to-all-start.1 = ((bf16[8,256,512]{1,2,0:T(8,128)(2,1)}), bf16[8,256,512]{1,2,0:T(8,128)(2,1)S(1)}, u32[]{:S(2)}, u32[]{:S(2)}) async-start(bf16[8,256,512]{1,2,0:T(8,128)(2,1)} %broadcast_in_dim.13), calls=%async_computation.2 | async-start | bytes 4194304 | tf_op jit(solution)/shard_map/all_to_all | solution.py:20
  284.7 0.1 copy.31
  284.8 25.5 %all-to-all-done.1 = bf16[8,256,512]{1,2,0:T(8,128)(2,1)S(1)} async-done(((bf16[8,256,512]{1,2,0:T(8,128)(2,1)}), bf16[8,256,512]{1,2,0:T(8,128)(2,1)S(1)}, u32[]{:S(2)}, u32[]{:S(2)}) %all-to-all-start.1) | async-done | bytes 2097184 | tf_op jit(solution)/shard_map/all_to_all | solution.py:20
  310.4 1.3 copy-done
  311.7 0.1 broadcast_in_dim.16
  311.8 29.5 %all_to_all.68 = bf16[8,256,512]{1,2,0:T(8,128)(2,1)S(1)} all-to-all(bf16[8,256,512]{1,2,0:T(8,128)(2,1)S(1)} %broadcast_in_dim.16), channel_id=1, replica_groups=mesh['tok'=16,'blk'=8] {'blk'}, dimensions={0} | all-to-all | bytes 4194304 | tf_op jit(solution)/shard_map/all_to_all | solution.py:20
  341.3 0.4 stack.4
  341.7 60.2 %all_to_all.69 = bf16[16,256,512]{2,1,0:T(8,128)(2,1)} all-to-all(bf16[16,256,512]{2,1,0:T(8,128)(2,1)S(1)} %stack.4), channel_id=1, replica_groups=mesh['tok'=16,'blk'=8] {'tok'}, dimensions={0} | all-to-all | bytes 8388608 | tf_op jit(solution)/shard_map/all_to_all | solution.py:50
  402.0 2.4 stack.5
  404.3 4.7 all-to-all-start.7
  409.1 4.9 fusion.8
  414.0 0.1 copy.28
  414.1 50.8 %all-to-all-done.7 = bf16[16,256,512]{2,1,0:T(8,128)(2,1)} async-done(((bf16[16,256,512]{2,1,0:T(8,128)(2,1)}), bf16[16,256,512]{2,1,0:T(8,128)(2,1)}, u32[]{:S(2)}, u32[]{:S(2)}) %all-to-all-start.7) | async-done | bytes 4194336 | tf_op jit(solution)/shard_map/all_to_all | solution.py:50
  464.9 1.5 broadcast_in_dim.14
  466.3 4.4 all-to-all-start.3
  470.7 3.5 fusion.9
  474.2 0.1 copy.32
  474.4 27.8 %all-to-all-done.3 = bf16[8,256,512]{1,2,0:T(8,128)(2,1)} async-done(((bf16[8,256,512]{1,2,0:T(8,128)(2,1)}), bf16[8,256,512]{1,2,0:T(8,128)(2,1)}, u32[]{:S(2)}, u32[]{:S(2)}) %all-to-all-start.3) | async-done | bytes 2097184 | tf_op jit(solution)/shard_map/all_to_all | solution.py:20
  502.1 1.5 broadcast_in_dim.17
  503.6 3.6 all-to-all-start.8
  507.2 5.0 fusion.2
  512.2 25.1 %all-to-all-done.8 = bf16[8,256,512]{1,2,0:T(8,128)(2,1)S(1)} async-done(((bf16[8,256,512]{1,2,0:T(8,128)(2,1)}), bf16[8,256,512]{1,2,0:T(8,128)(2,1)S(1)}, u32[]{:S(2)}, u32[]{:S(2)}) %all-to-all-start.8) | async-done | bytes 2097184 | tf_op jit(solution)/shard_map/all_to_all | solution.py:20
  537.3 3.4 all-to-all-start.4
  540.7 4.2 fusion.3
  545.0 4.1 all-to-all-done.4
  549.1 3.4 all-to-all-start.9
  552.5 0.1 convert_bitcast_fusion.1
  552.6 0.8 copy.34
  553.4 7.5 %all-to-all-done.9 = bf16[8,32,512]{2,1,0:T(8,128)(2,1)S(1)} async-done(((bf16[8,32,512]{2,1,0:T(8,128)(2,1)}), bf16[8,32,512]{2,1,0:T(8,128)(2,1)S(1)}, u32[]{:S(2)}, u32[]{:S(2)}) %all-to-all-start.9) | async-done | bytes 262176 | tf_op jit(solution)/shard_map/all_to_all | solution.py:99
  561.0 0.8 copy.35
  (12 shorter events, 0.1 us)
Async XLA Ops:
  7.2 125.1 %all-gather.2.cloned.1.call-start = ((), (), s32[]{:S(2)}) async-start(), calls=%async_computation.12 | async-start | bytes 9437184 | tf_op jit(solution)/shard_map/all_gather | solution.py:32
  9.6 197.6 %reduce-scatter.5.cloned.1.call-start = ((), (), s32[]{:S(2)}) async-start(), calls=%async_computation.14 | async-start | bytes 4456448 | tf_op jit(solution)/shard_map/reduce_scatter | solution.py:76
  138.9 1.0 copy-start.1
  138.9 136.1 %reduce-scatter.3.cloned.1.call-start = ((), (), s32[]{:S(2)}) async-start(), calls=%async_computation.13 | async-start | bytes 4456448 | tf_op jit(solution)/shard_map/reduce_scatter | solution.py:76
  153.7 11.1 %all-to-all-start.5 = ((bf16[16,2,2048]{2,1,0:T(2,128)(2,1)}), bf16[16,2,2048]{2,1,0:T(2,128)(2,1)S(1)}, u32[]{:S(2)}, u32[]{:S(2)}) async-start(bf16[16,2,2048]{2,1,0:T(2,128)(2,1)} %reshape.82), calls=%async_computation.7 | async-start | bytes 262144 | tf_op jit(solution)/shard_map/all_to_all | solution.py:20
  164.8 10.6 %all-to-all-start = ((bf16[16,2,2048]{2,1,0:T(2,128)(2,1)}), bf16[16,2,2048]{2,1,0:T(2,128)(2,1)S(1)}, u32[]{:S(2)}, u32[]{:S(2)}) async-start(bf16[16,2,2048]{2,1,0:T(2,128)(2,1)} %reshape.80), calls=%async_computation.1 | async-start | bytes 262144 | tf_op jit(solution)/shard_map/all_to_all | solution.py:20
  277.9 32.4 %all-to-all-start.1 = ((bf16[8,256,512]{1,2,0:T(8,128)(2,1)}), bf16[8,256,512]{1,2,0:T(8,128)(2,1)S(1)}, u32[]{:S(2)}, u32[]{:S(2)}) async-start(bf16[8,256,512]{1,2,0:T(8,128)(2,1)} %broadcast_in_dim.13), calls=%async_computation.2 | async-start | bytes 4194304 | tf_op jit(solution)/shard_map/all_to_all | solution.py:20
  310.4 1.3 copy-start
  404.3 60.5 %all-to-all-start.7 = ((bf16[16,256,512]{2,1,0:T(8,128)(2,1)}), bf16[16,256,512]{2,1,0:T(8,128)(2,1)}, u32[]{:S(2)}, u32[]{:S(2)}) async-start(bf16[16,256,512]{2,1,0:T(8,128)(2,1)} %stack.5), calls=%async_computation.9 | async-start | bytes 8388608 | tf_op jit(solution)/shard_map/all_to_all | solution.py:50
  466.3 35.8 %all-to-all-start.3 = ((bf16[8,256,512]{1,2,0:T(8,128)(2,1)}), bf16[8,256,512]{1,2,0:T(8,128)(2,1)}, u32[]{:S(2)}, u32[]{:S(2)}) async-start(bf16[8,256,512]{1,2,0:T(8,128)(2,1)} %broadcast_in_dim.14), calls=%async_computation.4 | async-start | bytes 4194304 | tf_op jit(solution)/shard_map/all_to_all | solution.py:20
  474.2 33.0 %copy-start.3 = (bf16[256,512]{1,0:T(8,128)(2,1)S(1)}, bf16[256,512]{1,0:T(8,128)(2,1)}, u32[]{:S(2)}) copy-start(bf16[256,512]{1,0:T(8,128)(2,1)} %reduce-scatter.3.cloned.1.call-done) | copy-start | bytes 786436
  503.6 33.7 %all-to-all-start.8 = ((bf16[8,256,512]{1,2,0:T(8,128)(2,1)}), bf16[8,256,512]{1,2,0:T(8,128)(2,1)S(1)}, u32[]{:S(2)}, u32[]{:S(2)}) async-start(bf16[8,256,512]{1,2,0:T(8,128)(2,1)} %broadcast_in_dim.17), calls=%async_computation.10 | async-start | bytes 4194304 | tf_op jit(solution)/shard_map/all_to_all | solution.py:20
  507.2 33.5 %copy-start.2 = (bf16[256,512]{1,0:T(8,128)(2,1)S(1)}, bf16[256,512]{1,0:T(8,128)(2,1)}, u32[]{:S(2)}) copy-start(bf16[256,512]{1,0:T(8,128)(2,1)} %reduce-scatter.5.cloned.1.call-done) | copy-start | bytes 786436
  537.3 11.8 %all-to-all-start.4 = ((bf16[8,32,512]{2,1,0:T(8,128)(2,1)}), bf16[8,32,512]{2,1,0:T(8,128)(2,1)S(1)}, u32[]{:S(2)}, u32[]{:S(2)}) async-start(bf16[8,32,512]{2,1,0:T(8,128)(2,1)} %bitcast.5), calls=%async_computation.5 | async-start | bytes 524288 | tf_op jit(solution)/shard_map/all_to_all | solution.py:99
  549.1 11.8 %all-to-all-start.9 = ((bf16[8,32,512]{2,1,0:T(8,128)(2,1)}), bf16[8,32,512]{2,1,0:T(8,128)(2,1)S(1)}, u32[]{:S(2)}, u32[]{:S(2)}) async-start(bf16[8,32,512]{2,1,0:T(8,128)(2,1)} %bitcast.12), calls=%async_computation.11 | async-start | bytes 524288 | tf_op jit(solution)/shard_map/all_to_all | solution.py:99
Sparse Core Ops, SparseCore 0:
  10.2 122.0 all-gather.1
  139.0 68.0 reduce-scatter.4
  209.5 65.4 reduce-scatter.2
